TPU v7x, 32 devices: a whole 2x2x4 slice. The times are simulated.
32 devices in a mesh: term: 8 (over z, core), sector: 4 (over y, x).
Axes of the slice: x: 2, y: 2, z: 4, core: 2. Of those that a mesh axis runs over, the one named last changes fastest.
Arguments:
- wavefunction: bfloat16 [24, 256, 256], P('sector'), may hold values from -6 to 6
- left_env: bfloat16 [24, 24, 256, 256], P('term', 'sector')
- right_env: bfloat16 [24, 24, 256, 256], P('term', 'sector')
- source: int32 [24, 24], P('term'), may hold values from 0 to 23, as said below
- block_size: int32 [24, 2], P('sector'), may hold values from 32 to 256
Outputs:
- first_product: float32 [24, 256, 256], P('sector', 'term')
- second_product: float32 [24, 256, 256], P('sector', 'term')
Inputs may be any that keep to these rules, and one draw needn't show every extreme that they name: Owner of sector s is s // 6. Among the 3 x 6 entries of source in one device's rows (one index of term) and columns (one index of sector), at most 5 name sectors of any one owner, and some owner is named exactly 5 times.
All inputs are finite; a program needn't handle non-finite values.
Results may differ from a plain program's by a relative error of at most 0.0037.
Values may be sent and summed in bfloat16 or wider, within the bound.
A program may use at most 64 MiB of HBM per device.

v0:
```python
import jax
import jax.numpy as jnp
from jax import lax
from jax.sharding import PartitionSpec as P

epsilon = 1e-06


def block_mask(block_size, width):
    positions = jnp.arange(width, dtype=jnp.int32)
    row_keep = positions[None, :] < block_size[:, 0:1]
    column_keep = positions[None, :] < block_size[:, 1:2]
    return row_keep[:, :, None] & column_keep[:, None, :]


def fetch_blocks(masked, source):
    local_count = masked.shape[0]
    width = masked.shape[1]
    bond_count = source.shape[0]
    my_index = lax.axis_index("sector")
    item_count = bond_count * local_count
    wanted = lax.dynamic_slice_in_dim(source, my_index * local_count, local_count, 1).reshape(
        item_count
    )
    pieces = lax.all_gather(masked, "sector", axis=0, tiled=True)
    piece_count = pieces.shape[0]
    numbers = jnp.arange(piece_count, dtype=jnp.int32)
    onehot = (wanted[:, None] == numbers[None, :]).astype(jnp.bfloat16)
    picked = jnp.dot(
        onehot, pieces.reshape(piece_count, width * width), preferred_element_type=jnp.float32
    )
    return picked.astype(jnp.bfloat16).reshape(bond_count, local_count, width, width)


def apply_operator(vector, left_env, right_env, source, keep):
    masked = jnp.where(keep, vector, jnp.zeros_like(vector))
    picked = fetch_blocks(masked, source)
    half_product = jnp.einsum(
        "bkij,bkjl->bkil", left_env, picked, preferred_element_type=jnp.float32
    ).astype(jnp.bfloat16)
    bond_terms = jnp.einsum(
        "bkil,bkml->bkim", half_product, right_env, preferred_element_type=jnp.float32
    )
    summed = jnp.sum(bond_terms, axis=0)
    return (jnp.where(keep, summed, jnp.zeros_like(summed)), masked)


def body(wavefunction, left_env, right_env, source, block_size):
    width = wavefunction.shape[1]
    keep = block_mask(block_size, width)
    term_count = lax.axis_size("term")
    term_index = lax.axis_index("term")
    row_count = width // term_count
    total_count = lax.axis_size("sector") * wavefunction.shape[0] * width * width
    partial_value, masked = apply_operator(wavefunction, left_env, right_env, source, keep)
    masked_float = masked.astype(jnp.float32)
    whole_sum = lax.psum(partial_value, "term")
    first_product = lax.dynamic_slice_in_dim(whole_sum, term_index * row_count, row_count, 1)
    margin, self_norm = lax.psum(
        (jnp.sum(masked_float * whole_sum), jnp.sum(masked_float * masked_float)), "sector"
    )
    residual = whole_sum - margin / self_norm * masked_float
    spread = lax.psum(jnp.sum(residual * residual), "sector")
    next_vector = (residual * lax.rsqrt(spread / total_count + epsilon)).astype(jnp.bfloat16)
    second_partial, _ = apply_operator(next_vector, left_env, right_env, source, keep)
    second_product = lax.psum_scatter(second_partial, "term", scatter_dimension=1, tiled=True)
    return (first_product, second_product)


def solution(mesh):
    placed = (
        P("sector", None, None),
        P("term", "sector", None, None),
        P("term", "sector", None, None),
        P("term", None),
        P("sector", None),
    )
    return jax.shard_map(
        body,
        mesh=mesh,
        in_specs=placed,
        out_specs=(P("sector", "term", None), P("sector", "term", None)),
        check_vma=False,
    )
```

profile of v0, /device:TPU:0, one launch (start us, length us, event | category | flops | bytes accessed | tf_op | source)
XLA Modules:
  0.0 256.0 jit_solution(13237176541998194756)
XLA Ops:
  7.2 0.0 copy-start
  7.2 0.0 copy-start.2
  7.2 0.0 all-gather.3.cloned.1.call-start
  7.2 0.9 slice_bitcast_fusion.1
  8.1 0.1 iota_compare_fusion.3
  8.2 2.3 and_select_fusion.3
  10.5 0.0 all-gather.3.cloned.1.call-update
  10.5 0.0 all-reduce.3.cloned.1.call-start
  10.6 0.0 copy-done.2
  10.6 0.1 constant_dynamic-slice_fusion.1
  10.7 0.1 eq.8
  10.8 46.5 %all-gather.3.cloned.1.call-done = bf16[24,256,256]{2,1,0:T(8,128)(2,1)} async-done(((bf16[6,256,256]{2,1,0:T(8,128)(2,1)}), bf16[24,256,256]{2,1,0:T(8,128)(2,1)}) %all-gather.3.cloned.1.call-update) | async-done | bytes 3145744 | tf_op jit(solution)/shard_map/all_gather | solution.py:25
  57.3 3.7 %copy.16 = bf16[3,8,256,256]{3,1,2,0:T(8,128)(2,1)S(1)} copy(bf16[3,8,256,256]{3,2,1,0:T(8,128)(2,1)} %bitcast.40) | data formatting | bytes 6291456
  60.9 1.0 convolution_convert_fusion.1
  62.0 0.7 copy.17
  62.7 1.7 slice.11
  64.4 0.0 copy-done
  64.4 0.0 copy-start.1
  64.4 5.0 %and_select_fusion.2 = f32[6,256,256]{2,1,0:T(8,128)} fusion(bf16[3,6,256,256]{3,2,1,0:T(8,128)(2,1)S(1)} %copy-done, bf16[3,6,256,256]{3,2,1,0:T(8,128)(2,1)} %bitcast.43, bf16[3,6,256,256]{3,2,1,0:T(8,128)(2,1)} %param.6, pred[6,256]{1,0:T(8,128)(4,1)S(1)} %get-tuple-element.8, pred[6,256]{1,0:T(8,128)(4,1)S(1)} %get-tuple-element.9), kind=kOutput, calls=%fused_computation.4 | convolution fusion | flops 1209925632 | bytes 8653824 | tf_op jit(solution)/shard_map/bkil,bkml->bkim/dot_general | solution.py:41
  69.4 0.0 all-reduce.3.cloned.1.call-update
  69.4 0.0 all-gather.5.cloned.1.call-start
  69.5 62.0 %all-reduce.3.cloned.1.call-done = f32[6,256,256]{2,1,0:T(8,128)} async-done(((f32[6,256,256]{2,1,0:T(8,128)}), f32[6,256,256]{2,1,0:T(8,128)}) %all-reduce.3.cloned.1.call-update) | async-done | bytes 1572880 | tf_op jit(solution)/shard_map/psum | solution.py:57
  131.5 0.0 copy-done.1
  131.5 2.6 %fusion.25 = (f32[]{:T(128)}, f32[]{:T(128)}) fusion(f32[6,256,256]{2,1,0:T(8,128)} %all-reduce.3.cloned.1.call-done, bf16[6,256,256]{2,1,0:T(8,128)(2,1)S(1)} %copy-done.1, pred[6,256]{1,0:T(8,128)(4,1)S(1)} %get-tuple-element.8, pred[6,256]{1,0:T(8,128)(4,1)S(1)} %get-tuple-element.9), kind=kLoop, calls=%fused_computation.24 | loop fusion | flops 2752510 | bytes 2362376 | tf_op jit(solution)/shard_map/reduce_sum | solution.py:60
  134.1 10.4 %all-reduce = (f32[]{:T(128)}, f32[]{:T(128)}) all-reduce(f32[]{:T(128)} %get-tuple-element.3, f32[]{:T(128)} %get-tuple-element.2), channel_id=1, replica_groups=mesh['term'=8,'sector'=4] {'sector'}, use_global_device_ids=true, to_apply=%region_2.3 | all-reduce | flops 2 | bytes 16 | tf_op jit(solution)/shard_map/psum | solution.py:59
  145.9 2.6 %multiply_reduce_fusion = f32[]{:T(128)} fusion(f32[6,256,256]{2,1,0:T(8,128)} %all-reduce.3.cloned.1.call-done, f32[]{:T(128)S(6)} %div.6, bf16[6,256,256]{2,1,0:T(8,128)(2,1)S(1)} %copy-done.1, pred[6,256]{1,0:T(8,128)(4,1)S(1)} %get-tuple-element.8, pred[6,256]{1,0:T(8,128)(4,1)S(1)} %get-tuple-element.9), kind=kLoop, calls=%fused_computation.27 | loop fusion | flops 2752511 | bytes 2362376 | tf_op jit(solution)/shard_map/reduce_sum | solution.py:63
  148.5 8.6 %psum.31 = f32[]{:T(128)} all-reduce(f32[]{:T(128)} %multiply_reduce_fusion), channel_id=1, replica_groups=mesh['term'=8,'sector'=4] {'sector'}, use_global_device_ids=true, to_apply=%region_6.7 | all-reduce | flops 1 | bytes 8 | tf_op jit(solution)/shard_map/psum | solution.py:63
  157.8 2.8 %and_select_fusion.1 = bf16[6,256,256]{2,1,0:T(8,128)(2,1)} fusion(f32[6,256,256]{2,1,0:T(8,128)} %all-reduce.3.cloned.1.call-done, f32[]{:T(128)S(6)} %rsqrt.3, f32[]{:T(128)S(6)} %div.6, pred[6,256]{1,0:T(8,128)(4,1)S(1)} %get-tuple-element.8, pred[6,256]{1,0:T(8,128)(4,1)S(1)} %get-tuple-element.9, bf16[6,256,256]{2,1,0:T(8,128)(2,1)S(1)} %copy-done.1), kind=kLoop, calls=%fused_computation.3 | loop fusion | flops 3145728 | bytes 3148808 | tf_op jit(solution)/shard_map/jit(_where)/select_n | solution.py:36
  160.6 0.0 all-gather.5.cloned.1.call-update
  160.6 0.2 reduce-scatter.2.cloned.1.call-start
  160.8 42.1 %all-gather.5.cloned.1.call-done = bf16[24,256,256]{2,1,0:T(8,128)(2,1)} async-done(((bf16[6,256,256]{2,1,0:T(8,128)(2,1)}), bf16[24,256,256]{2,1,0:T(8,128)(2,1)}) %all-gather.5.cloned.1.call-update) | async-done | bytes 3145744 | tf_op jit(solution)/shard_map/all_gather | solution.py:25
  203.0 3.7 %copy.18 = bf16[3,8,256,256]{3,1,2,0:T(8,128)(2,1)S(1)} copy(bf16[3,8,256,256]{3,2,1,0:T(8,128)(2,1)} %bitcast.41) | data formatting | bytes 6291456
  206.6 1.0 convolution_convert_fusion
  207.7 0.7 copy.19
  208.4 1.7 slice.12
  210.1 4.9 %and_select_fusion = f32[6,256,256]{2,1,0:T(8,128)} fusion(bf16[3,6,256,256]{3,2,1,0:T(8,128)(2,1)S(1)} %copy-done, bf16[3,6,256,256]{3,2,1,0:T(8,128)(2,1)} %bitcast.42, bf16[3,6,256,256]{3,2,1,0:T(8,128)(2,1)} %param.6, pred[6,256]{1,0:T(8,128)(4,1)S(1)} %get-tuple-element.8, pred[6,256]{1,0:T(8,128)(4,1)S(1)} %get-tuple-element.9), kind=kOutput, calls=%fused_computation.2 | convolution fusion | flops 1209925632 | bytes 8653824 | tf_op jit(solution)/shard_map/bkil,bkml->bkim/dot_general | solution.py:41
  215.0 0.0 reduce-scatter.2.cloned.1.call-update
  215.0 1.6 constant_dynamic-slice_fusion
  216.7 32.8 %reduce-scatter.2.cloned.1.call-done = f32[6,32,256]{2,1,0:T(8,128)} async-done(((f32[6,256,256]{2,1,0:T(8,128)}), f32[6,32,256]{2,1,0:T(8,128)}) %reduce-scatter.2.cloned.1.call-update) | async-done | bytes 196624 | tf_op jit(solution)/shard_map/reduce_scatter | solution.py:66
Async XLA Ops:
  7.2 57.2 %copy-start = (bf16[3,6,256,256]{3,2,1,0:T(8,128)(2,1)S(1)}, bf16[3,6,256,256]{3,2,1,0:T(8,128)(2,1)}, u32[]{:S(2)}) copy-start(bf16[3,6,256,256]{3,2,1,0:T(8,128)(2,1)} %param.7) | copy-start | bytes 7077892
  7.2 3.4 %copy-start.2 = (s32[3,24]{1,0:T(4,128)S(1)}, s32[3,24]{1,0:T(4,128)}, u32[]{:S(2)}) copy-start(s32[3,24]{1,0:T(4,128)} %param.8) | copy-start | bytes 868
  7.2 50.1 %all-gather.3.cloned.1.call-start = ((), (), s32[]{:S(2)}) async-start(), calls=%async_computation.1 | async-start | bytes 3932160 | tf_op jit(solution)/shard_map/all_gather | solution.py:25
  10.5 120.9 %all-reduce.3.cloned.1.call-start = ((), (), s32[]{:S(2)}) async-start(), calls=%async_computation.2 | async-start | bytes 3145728 | tf_op jit(solution)/shard_map/psum | solution.py:57
  64.4 67.1 %copy-start.1 = (bf16[6,256,256]{2,1,0:T(8,128)(2,1)S(1)}, bf16[6,256,256]{2,1,0:T(8,128)(2,1)}, u32[]{:S(2)}) copy-start(bf16[6,256,256]{2,1,0:T(8,128)(2,1)} %param.5) | copy-start | bytes 2359300
  69.4 133.6 %all-gather.5.cloned.1.call-start = ((), (), s32[]{:S(2)}) async-start(), calls=%async_computation.3 | async-start | bytes 3932160 | tf_op jit(solution)/shard_map/all_gather | solution.py:25
  160.6 88.8 %reduce-scatter.2.cloned.1.call-start = ((), (), s32[]{:S(2)}) async-start(), calls=%async_computation.4 | async-start | bytes 1769472 | tf_op jit(solution)/shard_map/reduce_scatter | solution.py:66
Sparse Core Ops, SparseCore 0:
  10.7 46.5 all-gather.2
  69.5 61.8 all-reduce.2
  160.7 42.1 all-gather.4
  215.1 34.2 reduce-scatter.1
where the time goes:
time: 256 us
  waiting for transfers between devices  183 us (71%)
  blocking collectives  19 us (7%)
  between operations  15.9 us (6%)
  local copies, waits for them, and re-layouts  14.8 us (6%)
  matrix products  12 us (5%)
  other arithmetic  10.5 us (4%)
    all_gather x2, waiting for transfers between devices, fetch_blocks(): pieces = lax.all_gather(masked, 'sector', axis=0, tiled=True)  88.6 us
    psum x1, waiting for transfers between devices, body(): whole_sum = lax.psum(partial_value, 'term')  62 us
    reduce_scatter x1, waiting for transfers between devices, body(): lax.psum_scatter(second_partial, 'term', scatter_dimension=1, tiled=True)  32.8 us
    unnamed x12, local copies, waits for them, and re-layouts  12.1 us
    psum x1, blocking collectives, body(): lax.psum((jnp.sum(masked_float * whole_sum), jnp.sum(masked_float * maske...  10.4 us
    dot_general x2, matrix products, apply_operator(): jnp.einsum('bkil,bkml->bkim', half_product, right_env, preferred_element_...  9.96 us
    psum x1, blocking collectives, body(): spread = lax.psum(jnp.sum(residual * residual), 'sector')  8.58 us
    select_n x2, other arithmetic, apply_operator(): masked = jnp.where(keep, vector, jnp.zeros_like(vector))  5.17 us
  transfers between devices with their start and end apart: 4, of which 4 were waited for; matrix products, arithmetic and copies ran while one was open for 1% of the time, Pallas kernels for 0%

commit v1 on v0

--- a/solution.py
+++ b/solution.py
@@ -22,7 +22,11 @@
     wanted = lax.dynamic_slice_in_dim(source, my_index * local_count, local_count, 1).reshape(
         item_count
     )
-    pieces = lax.all_gather(masked, "sector", axis=0, tiled=True)
+    frames = []
+    for _ in range(lax.axis_size("sector")):
+        frames.append(masked)
+    w_next = lax.all_to_all(jnp.stack(frames), split_axis=0, concat_axis=0, axis_name="sector")
+    pieces = jnp.concatenate(w_next, 0)
     piece_count = pieces.shape[0]
     numbers = jnp.arange(piece_count, dtype=jnp.int32)
     onehot = (wanted[:, None] == numbers[None, :]).astype(jnp.bfloat16)

time: 256 us -> 241 us (0.941)
  waiting for transfers between devices: 183 us -> 130 us
  blocking collectives: 19 us -> 52.9 us
  starting transfers between devices: 0.34 us -> 5.37 us
    all_gather x2 -> x0, waiting for transfers between devices: 88.6 us -> none  [fetch_blocks(): pieces = lax.all_gather(masked, 'sector', axis=0, tiled=True)]
    all_to_all x0 -> x1, waiting for transfers between devices: none -> 37 us  [fetch_blocks(): lax.all_to_all(jnp.stack(frames), split_axis=0, concat_axis=0, axis_name=...]
    all_to_all x0 -> x1, blocking collectives: none -> 33.9 us  [fetch_blocks(): lax.all_to_all(jnp.stack(frames), split_axis=0, concat_axis=0, axis_name=...]
    all_to_all x0 -> x1, starting transfers between devices: none -> 5.32 us  [fetch_blocks(): lax.all_to_all(jnp.stack(frames), split_axis=0, concat_axis=0, axis_name=...]
  transfers between devices with their start and end apart: 4 -> 3, of which waited for: 4 -> 3; matrix products, arithmetic and copies ran while one was open for 1% -> 1% of each run, Pallas kernels for 0% -> 0%
where the time goes in v1:
time: 241 us
  waiting for transfers between devices  130 us (54%)
  blocking collectives  52.9 us (22%)
  between operations  16.1 us (7%)
  local copies, waits for them, and re-layouts  15.2 us (6%)
  matrix products  12 us (5%)
  other arithmetic  8.73 us (4%)
  starting transfers between devices  5.37 us (2%)
    psum x1, waiting for transfers between devices, body(): whole_sum = lax.psum(partial_value, 'term')  62.5 us
    all_to_all x1, waiting for transfers between devices, fetch_blocks(): lax.all_to_all(jnp.stack(frames), split_axis=0, concat_axis=0, axis_name=...  37 us
    all_to_all x1, blocking collectives, fetch_blocks(): lax.all_to_all(jnp.stack(frames), split_axis=0, concat_axis=0, axis_name=...  33.9 us
    reduce_scatter x1, waiting for transfers between devices, body(): lax.psum_scatter(second_partial, 'term', scatter_dimension=1, tiled=True)  30.8 us
    psum x1, blocking collectives, body(): lax.psum((jnp.sum(masked_float * whole_sum), jnp.sum(masked_float * maske...  10.4 us
    unnamed x12, local copies, waits for them, and re-layouts  10.2 us
    dot_general x2, matrix products, apply_operator(): jnp.einsum('bkil,bkml->bkim', half_product, right_env, preferred_element_...  9.98 us
    psum x1, blocking collectives, body(): spread = lax.psum(jnp.sum(residual * residual), 'sector')  8.58 us
  transfers between devices with their start and end apart: 3, of which 3 were waited for; matrix products, arithmetic and copies ran while one was open for 1% of the time, Pallas kernels for 0%

profile of v1, /device:TPU:0, one launch (start us, length us, event | category | flops | bytes accessed | tf_op | source)
XLA Modules:
  0.0 240.6 jit_solution(7244490416886828420)
XLA Ops:
  7.2 0.0 copy-start
  7.2 0.8 slice_bitcast_fusion.1
  8.0 0.1 iota_compare_fusion.3
  8.1 1.5 and_select_fusion.3
  9.6 2.0 stack.4
  11.6 0.0 copy-start.2
  11.6 5.3 %all-to-all-start = ((bf16[4,6,256,256]{3,2,1,0:T(8,128)(2,1)}), bf16[4,6,256,256]{3,2,1,0:T(8,128)(2,1)}, u32[]{:S(2)}, u32[]{:S(2)}) async-start(bf16[4,6,256,256]{3,2,1,0:T(8,128)(2,1)} %stack.4), calls=%async_computation | async-start | bytes 6291456 | tf_op jit(solution)/shard_map/all_to_all | solution.py:28
  16.9 0.0 all-reduce.3.cloned.1.call-start
  17.0 0.0 copy-done.2
  17.0 0.1 constant_dynamic-slice_fusion.1
  17.0 0.1 eq.8
  17.1 37.0 %all-to-all-done = bf16[4,6,256,256]{3,2,1,0:T(8,128)(2,1)} async-done(((bf16[4,6,256,256]{3,2,1,0:T(8,128)(2,1)}), bf16[4,6,256,256]{3,2,1,0:T(8,128)(2,1)}, u32[]{:S(2)}, u32[]{:S(2)}) %all-to-all-start) | async-done | bytes 3145760 | tf_op jit(solution)/shard_map/all_to_all | solution.py:28
  54.1 3.7 %copy.14 = bf16[3,8,256,256]{3,1,2,0:T(8,128)(2,1)S(1)} copy(bf16[3,8,256,256]{3,2,1,0:T(8,128)(2,1)} %bitcast.9) | data formatting | bytes 6291456
  57.8 1.0 convolution_convert_fusion.1
  58.8 0.7 copy.15
  59.5 1.6 slice.11
  61.2 0.0 copy-done
  61.2 0.0 copy-start.1
  61.2 5.0 %and_select_fusion.2 = f32[6,256,256]{2,1,0:T(8,128)} fusion(bf16[3,6,256,256]{3,2,1,0:T(8,128)(2,1)S(1)} %copy-done, bf16[3,6,256,256]{3,2,1,0:T(8,128)(2,1)} %bitcast.44, bf16[3,6,256,256]{3,2,1,0:T(8,128)(2,1)} %param.6, pred[6,256]{1,0:T(8,128)(4,1)S(1)} %get-tuple-element.8, pred[6,256]{1,0:T(8,128)(4,1)S(1)} %get-tuple-element.9), kind=kOutput, calls=%fused_computation.4 | convolution fusion | flops 1209925632 | bytes 8653824 | tf_op jit(solution)/shard_map/bkil,bkml->bkim/dot_general | solution.py:45
  66.2 0.0 all-reduce.3.cloned.1.call-update
  66.2 0.0 reduce-scatter.2.cloned.1.call-start
  66.3 62.5 %all-reduce.3.cloned.1.call-done = f32[6,256,256]{2,1,0:T(8,128)} async-done(((f32[6,256,256]{2,1,0:T(8,128)}), f32[6,256,256]{2,1,0:T(8,128)}) %all-reduce.3.cloned.1.call-update) | async-done | bytes 1572880 | tf_op jit(solution)/shard_map/psum | solution.py:61
  128.8 0.0 copy-done.1
  128.8 2.6 %fusion.25 = (f32[]{:T(128)}, f32[]{:T(128)}) fusion(f32[6,256,256]{2,1,0:T(8,128)} %all-reduce.3.cloned.1.call-done, bf16[6,256,256]{2,1,0:T(8,128)(2,1)S(1)} %copy-done.1, pred[6,256]{1,0:T(8,128)(4,1)S(1)} %get-tuple-element.8, pred[6,256]{1,0:T(8,128)(4,1)S(1)} %get-tuple-element.9), kind=kLoop, calls=%fused_computation.24 | loop fusion | flops 2752510 | bytes 2362376 | tf_op jit(solution)/shard_map/reduce_sum | solution.py:64
  131.4 10.4 %all-reduce = (f32[]{:T(128)}, f32[]{:T(128)}) all-reduce(f32[]{:T(128)} %get-tuple-element.3, f32[]{:T(128)} %get-tuple-element.2), channel_id=1, replica_groups=mesh['term'=8,'sector'=4] {'sector'}, use_global_device_ids=true, to_apply=%region_2.3 | all-reduce | flops 2 | bytes 16 | tf_op jit(solution)/shard_map/psum | solution.py:63
  143.2 2.6 %multiply_reduce_fusion = f32[]{:T(128)} fusion(f32[6,256,256]{2,1,0:T(8,128)} %all-reduce.3.cloned.1.call-done, f32[]{:T(128)S(6)} %div.6, bf16[6,256,256]{2,1,0:T(8,128)(2,1)S(1)} %copy-done.1, pred[6,256]{1,0:T(8,128)(4,1)S(1)} %get-tuple-element.8, pred[6,256]{1,0:T(8,128)(4,1)S(1)} %get-tuple-element.9), kind=kLoop, calls=%fused_computation.27 | loop fusion | flops 2752511 | bytes 2362376 | tf_op jit(solution)/shard_map/reduce_sum | solution.py:67
  145.8 8.6 %psum.31 = f32[]{:T(128)} all-reduce(f32[]{:T(128)} %multiply_reduce_fusion), channel_id=1, replica_groups=mesh['term'=8,'sector'=4] {'sector'}, use_global_device_ids=true, to_apply=%region_6.7 | all-reduce | flops 1 | bytes 8 | tf_op jit(solution)/shard_map/psum | solution.py:67
  155.1 1.9 and_select_fusion.1
  157.1 0.3 stack.5
  157.4 33.9 %all_to_all.10 = bf16[4,6,256,256]{3,2,1,0:T(8,128)(2,1)S(1)} all-to-all(bf16[4,6,256,256]{3,2,1,0:T(8,128)(2,1)S(1)} %stack.5), channel_id=1, replica_groups=mesh['term'=8,'sector'=4] {'sector'}, dimensions={0} | all-to-all | bytes 6291456 | tf_op jit(solution)/shard_map/all_to_all | solution.py:28
  191.3 1.8 copy.16
  193.0 1.0 convolution_convert_fusion
  194.1 0.7 copy.17
  194.8 1.6 slice.12
  196.4 5.0 %and_select_fusion = f32[6,256,256]{2,1,0:T(8,128)} fusion(bf16[3,6,256,256]{3,2,1,0:T(8,128)(2,1)S(1)} %copy-done, bf16[3,6,256,256]{3,2,1,0:T(8,128)(2,1)} %bitcast.43, bf16[3,6,256,256]{3,2,1,0:T(8,128)(2,1)} %param.6, pred[6,256]{1,0:T(8,128)(4,1)S(1)} %get-tuple-element.8, pred[6,256]{1,0:T(8,128)(4,1)S(1)} %get-tuple-element.9), kind=kOutput, calls=%fused_computation.2 | convolution fusion | flops 1209925632 | bytes 8653824 | tf_op jit(solution)/shard_map/bkil,bkml->bkim/dot_general | solution.py:45
  201.4 0.0 reduce-scatter.2.cloned.1.call-update
  201.4 1.6 constant_dynamic-slice_fusion
  203.0 30.8 %reduce-scatter.2.cloned.1.call-done = f32[6,32,256]{2,1,0:T(8,128)} async-done(((f32[6,256,256]{2,1,0:T(8,128)}), f32[6,32,256]{2,1,0:T(8,128)}) %reduce-scatter.2.cloned.1.call-update) | async-done | bytes 196624 | tf_op jit(solution)/shard_map/reduce_scatter | solution.py:70
Async XLA Ops:
  7.2 54.0 %copy-start = (bf16[3,6,256,256]{3,2,1,0:T(8,128)(2,1)S(1)}, bf16[3,6,256,256]{3,2,1,0:T(8,128)(2,1)}, u32[]{:S(2)}) copy-start(bf16[3,6,256,256]{3,2,1,0:T(8,128)(2,1)} %param.7) | copy-start | bytes 7077892
  11.6 5.3 %copy-start.2 = (s32[3,24]{1,0:T(4,128)S(1)}, s32[3,24]{1,0:T(4,128)}, u32[]{:S(2)}) copy-start(s32[3,24]{1,0:T(4,128)} %param.8) | copy-start | bytes 868
  11.6 42.5 %all-to-all-start = ((bf16[4,6,256,256]{3,2,1,0:T(8,128)(2,1)}), bf16[4,6,256,256]{3,2,1,0:T(8,128)(2,1)}, u32[]{:S(2)}, u32[]{:S(2)}) async-start(bf16[4,6,256,256]{3,2,1,0:T(8,128)(2,1)} %stack.4), calls=%async_computation | async-start | bytes 6291456 | tf_op jit(solution)/shard_map/all_to_all | solution.py:28
  16.9 111.9 %all-reduce.3.cloned.1.call-start = ((), (), s32[]{:S(2)}) async-start(), calls=%async_computation.3 | async-start | bytes 3145728 | tf_op jit(solution)/shard_map/psum | solution.py:61
  61.2 67.6 %copy-start.1 = (bf16[6,256,256]{2,1,0:T(8,128)(2,1)S(1)}, bf16[6,256,256]{2,1,0:T(8,128)(2,1)}, u32[]{:S(2)}) copy-start(bf16[6,256,256]{2,1,0:T(8,128)(2,1)} %param.5) | copy-start | bytes 2359300
  66.2 167.6 %reduce-scatter.2.cloned.1.call-start = ((), (), s32[]{:S(2)}) async-start(), calls=%async_computation.4 | async-start | bytes 1769472 | tf_op jit(solution)/shard_map/reduce_scatter | solution.py:70
Sparse Core Ops, SparseCore 0:
  66.3 62.4 all-reduce.2
  201.5 32.2 reduce-scatter.1
